TPU v7x, 256 devices: a whole 4x4x8 slice. The times are simulated.
256 devices in a mesh: seq: 128 (over z, x, y), tp: 2 (over core).
Axes of the slice: x: 4, y: 4, z: 8, core: 2. Of those that a mesh axis runs over, the one named last changes fastest.
Arguments:
- img_qkv: bfloat16 [1, 4096, 3, 2048], P(None, 'seq', None, 'tp'), may hold values from -7 to 7
- txt_qkv: bfloat16 [1, 256, 3, 2048], P(None, None, None, 'tp'), may hold values from -7 to 7
- frame_index: int32 [1, 4096], P(None, 'seq'), may hold values from 0 to 32
- row_index: int32 [1, 4096], P(None, 'seq'), may hold values from 0 to 44
- column_index: int32 [1, 4096], P(None, 'seq'), may hold values from 0 to 79
- txt_len: int32 [1], replicated, may hold values from 64 to 256
- residual: bfloat16 [1, 4096, 3072], P(None, ('seq', 'tp')), may hold values from -6 to 6
- w_proj: bfloat16 [2048, 3072], P('tp'), may hold values from -0.125 to 0.125
- proj_bias: float32 [3072], replicated, may hold values from -3 to 3
- gate: float32 [3072], replicated, may hold values from -4 to 4
Outputs:
- img_out: bfloat16 [1, 4096, 3072], P(None, ('seq', 'tp'))
- txt_out: bfloat16 [1, 256, 2048], P(None, None, 'tp')
All inputs are finite; a program needn't handle non-finite values.
Results may differ from a plain program's by a relative error of at most 0.0082.
Values may be sent and summed in bfloat16 or wider, within the bound.
A program may use at most 64 MiB of HBM per device.

v0:
```python
import math

import jax
import jax.numpy as jnp
from jax import lax
from jax.sharding import Mesh
from jax.sharding import PartitionSpec as P

HD = 128
SEQ = ("seq_0", "seq_1", "seq_2")
SEQ_TP = ("seq_0", "seq_1", "seq_2", "tp")


rope_base = 256.0
neg_large = -1e30


def gathered_by_axis(x, axes, dim):
    for axis in reversed(axes):
        x = lax.all_gather(x, axis, axis=dim, tiled=True)
    return x


def copy_for_each(x, axis):
    size = lax.axis_size(axis)
    return lax.all_to_all(jnp.broadcast_to(x[None], (size, *x.shape)), axis, 0, 0, tiled=True)


def over_copies(x, axis):
    everything = copy_for_each(x, axis)
    return jnp.sum(everything.astype(jnp.float32), axis=0)


def rope_tables(frame_index, row_index, column_index, head_dim):
    frame_part = head_dim // 8
    second = (head_dim - frame_part) // 2
    pieces = []
    for places, part_width in (
        (frame_index, frame_part),
        (row_index, second),
        (column_index, second),
    ):
        pair_ids = jnp.arange(part_width // 2).astype(jnp.float32)
        pair_rates = rope_base ** (-2.0 * pair_ids / part_width)
        pieces.append(places.astype(jnp.float32)[:, None] * pair_rates[None, :])
    angles = jnp.repeat(jnp.concatenate(pieces, axis=1), 2, axis=1)
    parity = jnp.arange(head_dim) % 2
    signed = jnp.where(parity == 0, -1.0, 1.0).astype(jnp.float32)
    return (jnp.cos(angles), jnp.sin(angles) * signed[None, :])


def rotate(block_in, cosine, sine_table):
    values = block_in.astype(jnp.float32)
    parity = jnp.arange(values.shape[-1]) % 2
    partner = jnp.where(parity == 0, jnp.roll(values, -1, axis=-1), jnp.roll(values, 1, axis=-1))
    return (values * cosine[:, None, :] + partner * sine_table[:, None, :]).astype(jnp.bfloat16)


def absorb(carry_state, queries, block_keys, block_values, live_keys, score_scale):
    peak, weight_sum, blended = carry_state
    scores = (
        jnp.einsum("cqd,ckd->cqk", queries, block_keys, preferred_element_type=jnp.float32)
        * score_scale
    )
    if live_keys is not None:
        scores = jnp.where(live_keys[:, None, :], scores, neg_large)
    new_peak = jnp.maximum(peak, jnp.max(scores, axis=2))
    weights = jnp.exp(scores - new_peak[:, :, None])
    if live_keys is not None:
        weights = jnp.where(live_keys[:, None, :], weights, 0.0)
    shrink = jnp.exp(peak - new_peak)
    weight_sum = weight_sum * shrink + jnp.sum(weights, axis=2)
    blended = blended * shrink[:, :, None] + jnp.einsum(
        "cqk,ckd->cqd",
        weights.astype(jnp.bfloat16),
        block_values,
        preferred_element_type=jnp.float32,
    )
    return (new_peak, weight_sum, blended)


def shards(
    img_qkv,
    txt_qkv,
    frame_index,
    row_index,
    column_index,
    txt_len,
    residual,
    w_proj,
    proj_bias,
    gate,
):
    clips = img_qkv.shape[0]
    clip_tok = img_qkv.shape[1]
    head_dim = HD
    heads_tp = img_qkv.shape[3] // head_dim
    seq_count = lax.axis_size(SEQ)
    tp_count = lax.axis_size("tp")
    groups = seq_count // heads_tp
    per_group = clip_tok // groups
    txt_total = txt_qkv.shape[1]
    txt_share = txt_total // groups
    position = lax.axis_index(SEQ)
    my_head = position % heads_tp
    my_group = position // heads_tp
    score_scale = 1.0 / math.sqrt(head_dim)
    cosine, sine_table = rope_tables(
        frame_index.reshape(-1), row_index.reshape(-1), column_index.reshape(-1), head_dim
    )
    img_query = rotate(
        img_qkv[:, :, 0].reshape(clips * clip_tok, heads_tp, head_dim), cosine, sine_table
    ).reshape(clips, clip_tok, heads_tp, head_dim)
    img_key = rotate(
        img_qkv[:, :, 1].reshape(clips * clip_tok, heads_tp, head_dim), cosine, sine_table
    ).reshape(clips, clip_tok, heads_tp, head_dim)
    img_value = img_qkv[:, :, 2].reshape(clips, clip_tok, heads_tp, head_dim)
    query_send = (
        img_query.reshape(clips, groups, per_group, heads_tp, head_dim)
        .transpose(1, 3, 0, 2, 4)
        .reshape(seq_count, clips * per_group, head_dim)
    )
    key_value = jnp.stack([img_key, img_value], axis=2)
    txt_head = lax.dynamic_slice_in_dim(txt_qkv, my_head * head_dim, head_dim, 3)
    txt_query = lax.dynamic_slice_in_dim(txt_head[:, :, 0], my_group * txt_share, txt_share, 1)
    img_rows_count = seq_count * per_group
    query_rows = img_rows_count + txt_share
    start_state = (
        jnp.full((clips, query_rows), neg_large, jnp.float32),
        jnp.zeros((clips, query_rows), jnp.float32),
        jnp.zeros((clips, query_rows, head_dim), jnp.float32),
    )
    copies = jnp.broadcast_to(
        key_value.transpose(3, 0, 1, 2, 4)[None], (groups, heads_tp, clips, clip_tok, 2, head_dim)
    ).reshape(seq_count, clips, clip_tok, 2, head_dim)
    query_recv, pair_recv = (
        lax.all_to_all(query_send, SEQ, split_axis=0, concat_axis=0, tiled=True),
        lax.all_to_all(copies, SEQ, split_axis=0, concat_axis=0, tiled=True),
    )
    ordered = (
        query_recv.reshape(seq_count, clips, per_group, head_dim)
        .transpose(1, 0, 2, 3)
        .reshape(clips, img_rows_count, head_dim)
    )
    queries = jnp.concatenate([ordered, txt_query], axis=1)
    sources = max(1, min(seq_count, 2048 // clip_tok))
    while seq_count % sources:
        sources -= 1
    all_pairs = pair_recv.transpose(1, 0, 2, 3, 4).reshape(
        clips, seq_count // sources, sources * clip_tok, 2, head_dim
    )
    key_blocks = all_pairs.transpose(1, 0, 2, 3, 4)

    def sweep_block(carry_state, key_block):
        return (
            absorb(carry_state, queries, key_block[:, :, 0], key_block[:, :, 1], None, score_scale),
            None,
        )

    carry_state, unused = lax.scan(sweep_block, start_state, key_blocks)
    txt_live = jnp.arange(txt_total)[None, :] < txt_len[:, None]
    peak, weight_sum, blended = absorb(
        carry_state, queries, txt_head[:, :, 1], txt_head[:, :, 2], txt_live, score_scale
    )
    attended = (blended / weight_sum[:, :, None]).astype(jnp.bfloat16)
    img_part = (
        attended[:, :img_rows_count]
        .reshape(clips, seq_count, per_group, head_dim)
        .transpose(1, 0, 2, 3)
    )
    txt_part = attended[:, img_rows_count:]
    returned = lax.all_to_all(img_part, SEQ, split_axis=0, concat_axis=0, tiled=True)
    home_rows = (
        returned.reshape(groups, heads_tp, clips, per_group, head_dim)
        .transpose(2, 0, 3, 1, 4)
        .reshape(clips, clip_tok, heads_tp * head_dim)
    )
    txt_index = my_group * txt_share + jnp.arange(txt_share)
    txt_keep = (txt_index[None, :] < txt_len[:, None])[:, :, None]
    txt_part = jnp.where(txt_keep, txt_part, jnp.zeros_like(txt_part))
    gathered = gathered_by_axis(txt_part[None], SEQ, 0)
    txt_out = (
        gathered.reshape(groups, heads_tp, clips, txt_share, head_dim)
        .transpose(2, 0, 3, 1, 4)
        .reshape(clips, txt_total, heads_tp * head_dim)
    )
    row_share = clip_tok // tp_count
    share_rows = clips * row_share
    ordered_rows = (
        home_rows.reshape(clips, tp_count, row_share, heads_tp * head_dim)
        .transpose(1, 0, 2, 3)
        .reshape(tp_count * share_rows, heads_tp * head_dim)
    )
    full_sum = over_copies(
        jnp.dot(ordered_rows, w_proj, preferred_element_type=jnp.float32).astype(jnp.bfloat16), "tp"
    ).astype(jnp.float32)
    projected = lax.dynamic_slice_in_dim(full_sum, lax.axis_index("tp") * share_rows, share_rows, 0)
    projected = projected.reshape(clips, row_share, projected.shape[1])
    img_out = (
        residual.astype(jnp.float32) + gate[None, None, :] * (projected + proj_bias[None, None, :])
    ).astype(jnp.bfloat16)
    return (img_out, txt_out)


def solution(mesh):
    split = Mesh(mesh.devices.reshape(8, 4, 4, mesh.shape["tp"]), ("seq_0", "seq_1", "seq_2", "tp"))
    placed = (
        P(None, SEQ, None, "tp"),
        P(None, None, None, "tp"),
        P(None, SEQ),
        P(None, SEQ),
        P(None, SEQ),
        P(),
        P(None, SEQ_TP, None),
        P("tp", None),
        P(),
        P(),
    )
    return jax.shard_map(
        shards,
        mesh=split,
        in_specs=placed,
        out_specs=(P(None, SEQ_TP, None), P(None, None, "tp")),
        check_vma=False,
    )
```

profile of v0, /device:TPU:1, one launch (start us, length us, event | category | flops | bytes accessed | tf_op | source)
XLA Modules:
  0.0 180.9 jit_solution(878013164419484406)
XLA Ops:
  0.6 0.0 copy-start
  0.7 1.0 convert_bitcast_fusion.1
  1.8 0.1 fusion.41
  1.9 0.1 fusion.40
  2.0 0.7 convert_bitcast_fusion.4
  2.6 0.7 convert_bitcast_fusion.2
  3.3 0.1 broadcast_multiply_fusion.4
  3.4 0.1 broadcast_multiply_fusion.3
  3.5 0.2 fusion.37
  3.6 0.3 broadcast_in_dim.107
  3.9 0.6 sin.18
  4.5 0.3 broadcast_in_dim.105
  4.9 0.6 cos.18
  5.5 0.2 copy.90
  5.7 0.3 copy.80
  6.0 0.2 copy.91
  6.2 0.3 copy.82
  6.5 0.1 fusion.29
  6.7 0.7 copy.83
  7.4 16.3 %all-to-all-start.1 = ((bf16[128,2,128]{2,1,0:T(2,128)(2,1)}), bf16[128,2,128]{2,1,0:T(2,128)(2,1)S(1)}, u32[]{:S(2)}, u32[]{:S(2)}) async-start(bf16[128,2,128]{2,1,0:T(2,128)(2,1)} %bitcast.19), calls=%async_computation.1 | async-start | bytes 131072 | tf_op jit(solution)/shard_map/all_to_all | solution.py:137
  23.7 0.1 copy.93
  23.8 0.1 copy.92
  23.9 0.1 fusion.39
  24.0 0.1 slice_bitcast_fusion.4
  24.1 0.1 broadcast_multiply_fusion
  24.2 0.1 copy.75
  24.3 0.1 copy.69
  24.4 0.1 copy.70
  24.5 0.2 copy.71
  24.7 0.1 copy.72
  24.8 0.1 copy.73
  25.0 0.1 fusion.22
  25.2 9.2 %all-to-all-done.1 = bf16[128,2,128]{2,1,0:T(2,128)(2,1)S(1)} async-done(((bf16[128,2,128]{2,1,0:T(2,128)(2,1)}), bf16[128,2,128]{2,1,0:T(2,128)(2,1)S(1)}, u32[]{:S(2)}, u32[]{:S(2)}) %all-to-all-start.1) | async-done | bytes 65568 | tf_op jit(solution)/shard_map/all_to_all | solution.py:137
  34.4 1.8 %broadcast_in_dim.111 = bf16[16,8,32,2,128]{4,2,3,1,0:T(8,128)(2,1)} broadcast(bf16[8,32,2,128]{3,1,2,0:T(8,128)(2,1)S(1)} %copy.77), dimensions={1,2,3,4} | broadcast | bytes 2228224 | tf_op jit(solution)/shard_map/broadcast_in_dim | solution.py:133
  36.2 7.3 %all-to-all-start = ((bf16[128,1,32,2,128]{4,2,3,1,0:T(8,128)(2,1)}), bf16[128,1,32,2,128]{4,2,3,1,0:T(8,128)(2,1)}, u32[]{:S(2)}, u32[]{:S(2)}) async-start(bf16[128,1,32,2,128]{4,2,3,1,0:T(8,128)(2,1)} %bitcast.143), calls=%async_computation | async-start | bytes 4194304 | tf_op jit(solution)/shard_map/all_to_all | solution.py:138
  44.4 0.3 fusion.42
  44.7 46.9 %all-to-all-done = bf16[128,1,32,2,128]{4,2,3,1,0:T(8,128)(2,1)} async-done(((bf16[128,1,32,2,128]{4,2,3,1,0:T(8,128)(2,1)}), bf16[128,1,32,2,128]{4,2,3,1,0:T(8,128)(2,1)}, u32[]{:S(2)}, u32[]{:S(2)}) %all-to-all-start) | async-done | bytes 2097184 | tf_op jit(solution)/shard_map/all_to_all | solution.py:138
  91.6 3.3 %copy.78 = bf16[128,1,32,2,128]{4,2,0,3,1:T(8,128)(2,1)} copy(bf16[128,1,32,2,128]{4,2,3,1,0:T(8,128)(2,1)} %all-to-all-done) | data formatting | bytes 4194304 | tf_op jit(solution)/shard_map/all_to_all | solution.py:138
  94.9 12.0 %while.15 = (s32[]{:T(128)}, f32[1,272]{1,0:T(1,128)S(1)}, f32[1,272]{1,0:T(1,128)S(1)}, f32[1,272,128]{2,1,0:T(8,128)S(1)}, bf16[2,1,2048,2,128]{4,2,0,3,1:T(8,...) while((s32[]{:T(128)}, f32[1,272]{1,0:T(1,128)S(1)}, ...), condition=%wide.region_3.4_spmd.clone, body=%wide.region_0.3_spmd.clone.sunk | while | flops 288661088 | bytes 19112000 | solution.py:160
  94.9 1.3 dynamic-slice_bitcast_fusion.7
  96.2 1.9 %fusion.51 = (f32[272]{0:T(512)S(1)}, f32[2048,272]{0,1:T(8,128)}) fusion(bf16[1,272,128]{2,1,0:T(8,128)(2,1)S(1)} %get-tuple-element.184, bf16[1,2048,2,128]{3,1,2,0:T(8,128)(2,1)S(1)} %dynamic-slice_bitcast_fusion.7), kind=kOutput, calls=%fused_computation.85.clone.1 | convolution fusion | flops 143720176 | bytes 2823232 | tf_op jit(solution)/shard_map/while/body/eval_jaxpr/cqd,ckd->cqk/dot_general | solution.py:62
  98.0 2.3 %fusion.55 = f32[1,272,128]{2,1,0:T(8,128)S(1)} fusion(f32[2048,272]{0,1:T(8,128)} %get-tuple-element.160, f32[272]{0:T(512)S(1)} %get-tuple-element.161, bf16[1,2048,2,128]{3,1,2,0:T(8,128)(2,1)S(1)} %dynamic-slice_bitcast_fusion.7, f32[1,272,128]{2,1,0:T(8,128)S(1)} %get-tuple-element.174, f32[272]{0:T(512)S(1)} %get-tuple-element.162, pred[]{:T(512)S(6)} %compare.8), kind=kOutput, calls=%fused_computation.5.clone.1 | convolution fusion | flops 143824896 | bytes 3035137 | tf_op jit(solution)/shard_map/while/body/eval_jaxpr/cqk,ckd->cqd/dot_general | solution.py:73
  100.3 0.5 fusion.53
  100.9 1.3 dynamic-slice_bitcast_fusion.7
  102.2 1.9 %fusion.51 = (f32[272]{0:T(512)S(1)}, f32[2048,272]{0,1:T(8,128)}) fusion(bf16[1,272,128]{2,1,0:T(8,128)(2,1)S(1)} %get-tuple-element.184, bf16[1,2048,2,128]{3,1,2,0:T(8,128)(2,1)S(1)} %dynamic-slice_bitcast_fusion.7), kind=kOutput, calls=%fused_computation.85.clone.1 | convolution fusion | flops 143720176 | bytes 2823232 | tf_op jit(solution)/shard_map/while/body/eval_jaxpr/cqd,ckd->cqk/dot_general | solution.py:62
  104.1 2.3 %fusion.55 = f32[1,272,128]{2,1,0:T(8,128)S(1)} fusion(f32[2048,272]{0,1:T(8,128)} %get-tuple-element.160, f32[272]{0:T(512)S(1)} %get-tuple-element.161, bf16[1,2048,2,128]{3,1,2,0:T(8,128)(2,1)S(1)} %dynamic-slice_bitcast_fusion.7, f32[1,272,128]{2,1,0:T(8,128)S(1)} %get-tuple-element.174, f32[272]{0:T(512)S(1)} %get-tuple-element.162, pred[]{:T(512)S(6)} %compare.8), kind=kOutput, calls=%fused_computation.5.clone.1 | convolution fusion | flops 143824896 | bytes 3035137 | tf_op jit(solution)/shard_map/while/body/eval_jaxpr/cqk,ckd->cqd/dot_general | solution.py:73
  106.4 0.5 fusion.53
  106.9 0.2 fusion.13
  107.2 0.2 fusion.12
  107.4 0.6 slice.86
  108.0 0.1 slice_select_fusion
  108.1 9.1 %all-gather = bf16[4,16,128]{2,1,0:T(8,128)(2,1)S(1)} all-gather(bf16[1,16,128]{2,1,0:T(8,128)(2,1)S(1)} %slice_select_fusion), channel_id=2, replica_groups=mesh['seq_0'=8,'seq_1'=4,'seq_2'=4,'tp'=2] {'seq_2'}, dimensions={0}, use_global_device_ids=true | all-gather | bytes 20480 | tf_op jit(solution)/shard_map/all_gather | solution.py:20
  117.2 9.0 %all-gather.1 = bf16[16,16,128]{2,1,0:T(8,128)(2,1)S(1)} all-gather(bf16[4,16,128]{2,1,0:T(8,128)(2,1)S(1)} %all-gather), channel_id=3, replica_groups=mesh['seq_0'=8,'seq_1'=4,'seq_2'=4,'tp'=2] {'seq_1'}, dimensions={0}, use_global_device_ids=true | all-gather | bytes 81920 | tf_op jit(solution)/shard_map/all_gather | solution.py:20
  126.2 11.2 %all-to-all-start.2 = ((bf16[128,1,2,128]{3,2,1,0:T(2,128)(2,1)}), bf16[128,1,2,128]{3,2,1,0:T(2,128)(2,1)S(1)}, u32[]{:S(2)}, u32[]{:S(2)}) async-start(bf16[128,1,2,128]{3,2,1,0:T(2,128)(2,1)} %bitcast.28), calls=%async_computation.2 | async-start | bytes 131072 | tf_op jit(solution)/shard_map/all_to_all | solution.py:172
  137.4 20.6 %all-gather.2 = bf16[128,16,128]{2,1,0:T(8,128)(2,1)S(1)} all-gather(bf16[16,16,128]{2,1,0:T(8,128)(2,1)S(1)} %all-gather.1), channel_id=4, replica_groups=mesh['seq_0'=8,'seq_1'=4,'seq_2'=4,'tp'=2] {'seq_0'}, dimensions={0}, use_global_device_ids=true | all-gather | bytes 589824 | tf_op jit(solution)/shard_map/all_gather | solution.py:20
  158.1 0.1 copy.88
  158.2 1.0 reshape.362
  159.3 0.0 copy-start.3
  159.3 0.0 copy-start.4
  159.3 4.0 %convolution_convert_fusion = bf16[32,3072]{1,0:T(8,128)(2,1)S(1)} fusion(bf16[1024,3072]{1,0:T(8,128)(2,1)} %param.19, bf16[4,8,8,128]{3,2,1,0:T(8,128)(2,1)S(1)} %bitcast.155), kind=kOutput, calls=%fused_computation.19 | convolution fusion | flops 201424896 | bytes 6553600 | tf_op jit(solution)/shard_map/dot_general | solution.py:195
  163.3 0.0 copy-start.2
  163.3 16.8 %all_to_all.20 = bf16[2,32,3072]{2,1,0:T(8,128)(2,1)S(1)} all-to-all(bf16[2,32,3072]{2,1,0:T(8,128)(2,1)S(1)} %broadcast_in_dim.117), channel_id=1, replica_groups=mesh['seq_0'=8,'seq_1'=4,'seq_2'=4,'tp'=2] {'tp'}, dimensions={0} | all-to-all | bytes 786432 | tf_op jit(solution)/shard_map/all_to_all | solution.py:26
  180.1 0.1 convert_reduce_fusion
  180.2 0.7 fusion.15
  (39 shorter events, 0.5 us)
Async XLA Ops:
  0.6 43.7 %copy-start = (bf16[1,256,3,1024]{3,1,2,0:T(8,128)(2,1)S(1)}, bf16[1,256,3,1024]{3,1,2,0:T(8,128)(2,1)}, u32[]{:S(2)}) copy-start(bf16[1,256,3,1024]{3,1,2,0:T(8,128)(2,1)} %param.13) | copy-start | bytes 4718596
  7.4 27.0 %all-to-all-start.1 = ((bf16[128,2,128]{2,1,0:T(2,128)(2,1)}), bf16[128,2,128]{2,1,0:T(2,128)(2,1)S(1)}, u32[]{:S(2)}, u32[]{:S(2)}) async-start(bf16[128,2,128]{2,1,0:T(2,128)(2,1)} %bitcast.19), calls=%async_computation.1 | async-start | bytes 131072 | tf_op jit(solution)/shard_map/all_to_all | solution.py:137
  36.2 55.4 %all-to-all-start = ((bf16[128,1,32,2,128]{4,2,3,1,0:T(8,128)(2,1)}), bf16[128,1,32,2,128]{4,2,3,1,0:T(8,128)(2,1)}, u32[]{:S(2)}, u32[]{:S(2)}) async-start(bf16[128,1,32,2,128]{4,2,3,1,0:T(8,128)(2,1)} %bitcast.143), calls=%async_computation | async-start | bytes 4194304 | tf_op jit(solution)/shard_map/all_to_all | solution.py:138
  98.0 2.3 %copy-start.1 = (f32[2048,272]{0,1:T(8,128)S(1)}, f32[2048,272]{0,1:T(8,128)}, u32[]{:S(2)}) copy-start(f32[2048,272]{0,1:T(8,128)} %get-tuple-element.160) | copy-start | bytes 6684676 | tf_op jit(solution)/shard_map/while
  104.0 2.3 %copy-start.1 = (f32[2048,272]{0,1:T(8,128)S(1)}, f32[2048,272]{0,1:T(8,128)}, u32[]{:S(2)}) copy-start(f32[2048,272]{0,1:T(8,128)} %get-tuple-element.160) | copy-start | bytes 6684676 | tf_op jit(solution)/shard_map/while
  126.2 33.0 %all-to-all-start.2 = ((bf16[128,1,2,128]{3,2,1,0:T(2,128)(2,1)}), bf16[128,1,2,128]{3,2,1,0:T(2,128)(2,1)S(1)}, u32[]{:S(2)}, u32[]{:S(2)}) async-start(bf16[128,1,2,128]{3,2,1,0:T(2,128)(2,1)} %bitcast.28), calls=%async_computation.2 | async-start | bytes 131072 | tf_op jit(solution)/shard_map/all_to_all | solution.py:172
  159.3 20.9 %copy-start.3 = (f32[3072]{0:T(1024)S(1)}, f32[3072]{0:T(1024)}, u32[]{:S(2)}) copy-start(f32[3072]{0:T(1024)} %param.20) | copy-start | bytes 36868
  159.3 20.9 %copy-start.4 = (f32[3072]{0:T(1024)S(1)}, f32[3072]{0:T(1024)}, u32[]{:S(2)}) copy-start(f32[3072]{0:T(1024)} %param.21) | copy-start | bytes 36868
  163.3 16.9 %copy-start.2 = (bf16[1,16,3072]{2,1,0:T(8,128)(2,1)S(1)}, bf16[1,16,3072]{2,1,0:T(8,128)(2,1)}, u32[]{:S(2)}) copy-start(bf16[1,16,3072]{2,1,0:T(8,128)(2,1)} %param.18) | copy-start | bytes 294916
where the time goes:
time: 181 us
  waiting for transfers between devices  56.1 us (31%)
  blocking collectives  55.5 us (31%)
  starting transfers between devices  34.9 us (19%)
  local copies, waits for them, and re-layouts  14.5 us (8%)
  matrix products  12.8 us (7%)
  other arithmetic  5.25 us (3%)
    all_to_all x1, waiting for transfers between devices, shards(): lax.all_to_all(copies, SEQ, split_axis=0, concat_axis=0, tiled=True)  46.9 us
    all_gather x3, blocking collectives, gathered_by_axis(): x = lax.all_gather(x, axis, axis=dim, tiled=True)  38.7 us
    all_to_all x1, blocking collectives, copy_for_each(): lax.all_to_all(jnp.broadcast_to(x[None], (size, *x.shape)), axis, 0, 0, t...  16.8 us
    all_to_all x1, starting transfers between devices, shards(): lax.all_to_all(query_send, SEQ, split_axis=0, concat_axis=0, tiled=True)  16.3 us
    all_to_all x1, starting transfers between devices, shards(): lax.all_to_all(img_part, SEQ, split_axis=0, concat_axis=0, tiled=True)  11.2 us
    all_to_all x1, waiting for transfers between devices, shards(): lax.all_to_all(query_send, SEQ, split_axis=0, concat_axis=0, tiled=True)  9.19 us
    all_to_all x1, starting transfers between devices, shards(): lax.all_to_all(copies, SEQ, split_axis=0, concat_axis=0, tiled=True)  7.34 us
    dot_general x3, matrix products, absorb(): jnp.einsum('cqk,ckd->cqd', weights.astype(jnp.bfloat16), block_values, pr...  4.82 us
  transfers between devices with their start and end apart: 3, of which 2 were waited for; matrix products, arithmetic and copies ran while one was open for 2% of the time, Pallas kernels for 0%

commit v1 on v0

v1 whole, which is shorter than its diff:
```python
import math

import jax
import jax.numpy as jnp
from jax import lax
from jax.experimental import pallas as pl
from jax.experimental.pallas import tpu as pltpu
from jax.sharding import Mesh
from jax.sharding import PartitionSpec as P

HD = 128
AX_Z, AX_X, AX_Y, AX_C = "seq_0", "seq_1", "seq_2", "tp"
SEQ = (AX_Z, AX_X, AX_Y)
SEQ_TP = (AX_Z, AX_X, AX_Y, AX_C)
MESH = pl.DeviceIdType.MESH
F32 = jnp.float32
BF16 = jnp.bfloat16

rope_base = 256.0
neg_large = -1e30


def rope_in_kernel(frames, rows, columns, tok):
    part0 = HD // 8
    part1 = (HD - part0) // 2
    eye = lax.broadcasted_iota(jnp.int32, (tok, tok), 0) == lax.broadcasted_iota(jnp.int32, (tok, tok), 1)

    def column(ref):
        places = jnp.broadcast_to(ref[...].astype(F32), (tok, tok))
        return jnp.sum(jnp.where(eye, places, 0.0), axis=1, keepdims=True)

    lane = lax.broadcasted_iota(jnp.int32, (tok, HD), 1)
    in0 = lane < part0
    in1 = lane < part0 + part1
    start = jnp.where(in0, 0, jnp.where(in1, part0, part0 + part1))
    pair = ((lane - start) >> 1).astype(F32)
    width = jnp.where(in0, float(part0), float(part1))
    rate = jnp.exp(pair * (-2.0 * math.log(rope_base)) / width)
    place = jnp.where(in0, column(frames), jnp.where(in1, column(rows), column(columns)))
    angle = place * rate
    cosine, sine = jnp.cos(angle), jnp.sin(angle)
    even = (lane & 1) == 0
    return cosine, jnp.where(even, -sine, 0.0), jnp.where(even, 0.0, sine)


def kernel_body(
    Z, X, Y, tok,
    qkv_hbm, txt_hbm, w_hbm, frames, rows, columns, txt_len,
    p_out, t_out,
    qkv_v, w_v, tq, tk, tv, send, qg, kvg, ob, st, orecv, srecv, tob, tst, torecv, tsrecv,
    zs, ar, tbuf, part_own, part_send, part_recv,
    local_sem, zq_sem, zkv_sem, z_send, xq_sem, xq_send, ykv_sem, ykv_send,
    xo_sem, xs_sem, xo_send, xs_send, xto_sem, xts_sem, xto_send, xts_send,
    zo_sem, zo_send, t2_sem, t2_send, t3_sem, t3_send, c_sem, c_send,
):
    z, x, y, c = (lax.axis_index(a) for a in SEQ_TP)
    txt_q = tq.shape[0]
    txt_k = tk.shape[0]
    scale2 = math.log2(math.e) / math.sqrt(HD)

    def put(src, dst, ssem, rsem, axis, to):
        pltpu.make_async_remote_copy(
            src_ref=src, dst_ref=dst, send_sem=ssem, recv_sem=rsem,
            device_id={axis: to}, device_id_type=MESH,
        ).start()

    def await_bytes(ref, sem):
        pltpu.make_async_copy(ref, ref, sem).wait()

    barrier = pltpu.get_barrier_semaphore()
    peers = 0
    for axis, size, me in ((AX_Z, Z, z), (AX_X, X, x), (AX_Y, Y, y), (AX_C, 2, c)):
        for step in range(1, size):
            pl.semaphore_signal(barrier, inc=1, device_id={axis: lax.rem(me + step, size)}, device_id_type=MESH)
            peers += 1

    lane0 = pl.multiple_of(z * HD, HD)
    get_qkv = pltpu.make_async_copy(qkv_hbm, qkv_v, local_sem.at[0])
    get_qkv.start()
    get_tq = pltpu.make_async_copy(
        txt_hbm.at[0, pl.ds(pl.multiple_of(y * txt_q, txt_q), txt_q), pl.ds(lane0, HD)], tq, local_sem.at[1])
    get_tk = pltpu.make_async_copy(
        txt_hbm.at[1, pl.ds(pl.multiple_of(x * txt_k, txt_k), txt_k), pl.ds(lane0, HD)], tk, local_sem.at[2])
    get_tv = pltpu.make_async_copy(
        txt_hbm.at[2, pl.ds(pl.multiple_of(x * txt_k, txt_k), txt_k), pl.ds(lane0, HD)], tv, local_sem.at[3])
    get_w = pltpu.make_async_copy(w_hbm, w_v, local_sem.at[4])
    for get in (get_tq, get_tk, get_tv, get_w):
        get.start()

    cosine, sine_even, sine_odd = rope_in_kernel(frames, rows, columns, tok)
    get_qkv.wait()
    for h in range(Z):
        lanes = slice(h * HD, (h + 1) * HD)
        for kind in range(2):
            block = qkv_v[kind, :, lanes].astype(F32)
            turned = (
                block * cosine
                + pltpu.roll(block, HD - 1, 1) * sine_even
                + pltpu.roll(block, 1, 1) * sine_odd
            )
            send[h, kind] = turned.astype(BF16)
        send[h, 2] = qkv_v[2, :, lanes]
    qg[x, z] = send[z, 0]
    kvg[y, z] = send[z, 1:3]

    pl.semaphore_wait(barrier, peers)

    order = sorted(range(1, Z), key=lambda step: -min(step, Z - step))
    for step in order:
        to = lax.rem(z + step, Z)
        put(send.at[to, 1:3], kvg.at[y, z], z_send, zkv_sem.at[z], AX_Z, to)
        put(send.at[to, 0], qg.at[x, z], z_send, zq_sem.at[z], AX_Z, to)

    for step in [0] + order:
        source = lax.rem(z + step, Z)
        if step:
            await_bytes(kvg.at[y, source], zkv_sem.at[source])
        for hop in range(1, Y):
            put(kvg.at[y, source], kvg.at[y, source], ykv_send, ykv_sem.at[y], AX_Y, lax.rem(y + hop, Y))
        if step:
            await_bytes(qg.at[x, source], zq_sem.at[source])
        for hop in range(1, X):
            put(qg.at[x, source], qg.at[x, source], xq_send, xq_sem.at[x], AX_X, lax.rem(x + hop, X))

    for get in (get_tq, get_tk, get_tv):
        get.wait()
    for hop in range(1, Y):
        other = lax.rem(y + hop, Y)
        await_bytes(kvg.at[other], ykv_sem.at[other])
    for hop in range(1, X):
        other = lax.rem(x + hop, X)
        await_bytes(qg.at[other], xq_sem.at[other])

    keys_n = Y * Z * tok
    live = lax.broadcasted_iota(jnp.int32, (1, txt_k), 1) < txt_len[0] - x * txt_k

    def scores_of(queries, keys):
        return lax.dot_general(queries, keys, (((1,), (1,)), ((), ())), preferred_element_type=F32)

    def attend(queries):
        scores = scores_of(queries, kvg[:, :, 0].reshape(keys_n, HD))
        txt_scores = jnp.where(live, scores_of(queries, tk[...]), neg_large)
        peak = jnp.maximum(
            jnp.max(scores, axis=1, keepdims=True), jnp.max(txt_scores, axis=1, keepdims=True))
        weights = jnp.exp2((scores - peak) * scale2)
        txt_weights = jnp.exp2((txt_scores - peak) * scale2)
        total = jnp.sum(weights, axis=1, keepdims=True) + jnp.sum(txt_weights, axis=1, keepdims=True)
        blended = jnp.dot(
            weights.astype(BF16), kvg[:, :, 1].reshape(keys_n, HD), preferred_element_type=F32)
        blended += jnp.dot(txt_weights.astype(BF16), tv[...], preferred_element_type=F32)
        return blended / total, peak * scale2 + jnp.log2(total)

    def to_row(col):
        n = col.shape[0]
        eye = lax.broadcasted_iota(jnp.int32, (n, HD), 0) == lax.broadcasted_iota(jnp.int32, (n, HD), 1)
        return jnp.sum(jnp.where(eye, jnp.broadcast_to(col, (n, HD)), 0.0), axis=0, keepdims=True)

    def to_col(row, n):
        eye = lax.broadcasted_iota(jnp.int32, (n, HD), 0) == lax.broadcasted_iota(jnp.int32, (n, HD), 1)
        return jnp.sum(jnp.where(eye, jnp.broadcast_to(row, (n, HD)), 0.0), axis=1, keepdims=True)

    def merge(values, logs):
        top = logs[0]
        for log in logs[1:]:
            top = jnp.maximum(top, log)
        shares = [jnp.exp2(log - top) for log in logs]
        return sum(v * s for v, s in zip(values, shares)) / sum(shares)

    part, log = attend(tq[...])
    tob[...] = part.astype(BF16)
    tst[...] = to_row(log)
    for hop in range(1, X):
        to = lax.rem(x + hop, X)
        put(tob, torecv.at[x], xto_send.at[hop], xto_sem.at[x], AX_X, to)
        put(tst, tsrecv.at[x], xts_send.at[hop], xts_sem.at[x], AX_X, to)

    block_n = Z * tok
    strips = block_n // HD
    for hop in sorted(range(1, X), key=lambda hop: -min(hop, X - hop)) + [0]:
        to = lax.rem(x + hop, X)
        part, log = attend(qg[to].reshape(block_n, HD))
        ob[to] = part.astype(BF16)
        for strip in range(strips):
            st[to, strip] = to_row(log[strip * HD:(strip + 1) * HD])
        if hop:
            put(ob.at[to], orecv.at[x], xo_send.at[hop], xo_sem.at[x], AX_X, to)
            put(st.at[to], srecv.at[x], xs_send.at[hop], xs_sem.at[x], AX_X, to)

    values, logs = [tob[...].astype(F32)], [to_col(tst[...], txt_q)]
    for hop in range(1, X):
        other = lax.rem(x + hop, X)
        await_bytes(torecv.at[other], xto_sem.at[other])
        await_bytes(tsrecv.at[other], xts_sem.at[other])
        values.append(torecv[other].astype(F32))
        logs.append(to_col(tsrecv[other], txt_q))
    kept = lax.broadcasted_iota(jnp.int32, (txt_q, 1), 0) + y * txt_q < txt_len[0]
    tbuf[y, z] = jnp.where(kept, merge(values, logs), 0.0).astype(BF16)

    values, logs = [ob[x].astype(F32)], [[to_col(st[x, strip], HD) for strip in range(strips)]]
    for hop in range(1, X):
        other = lax.rem(x + hop, X)
        await_bytes(orecv.at[other], xo_sem.at[other])
        await_bytes(srecv.at[other], xs_sem.at[other])
        values.append(orecv[other].astype(F32))
        logs.append([to_col(srecv[other, strip], HD) for strip in range(strips)])
    for strip in range(strips):
        rows_at = slice(strip * HD, (strip + 1) * HD)
        mixed = merge([v[rows_at] for v in values], [g[strip] for g in logs]).astype(BF16)
        per = HD // tok
        zs[strip * per:(strip + 1) * per] = mixed.reshape(per, tok, HD)
    ar[z] = zs[z]
    for step in order:
        to = lax.rem(z + step, Z)
        put(zs.at[to], ar.at[z], zo_send, zo_sem, AX_Z, to)
    for step in order:
        to = lax.rem(z + step, Z)
        put(tbuf.at[y, z], tbuf.at[y, z], t2_send, t2_sem, AX_Z, to)

    await_bytes(ar.at[0:Z - 1], zo_sem)
    get_w.wait()
    mine = jnp.concatenate([ar[h] for h in range(Z)], axis=1)
    half = tok // 2
    cuts = part_send.shape[0]
    wide = part_send.shape[2]
    for cut in range(cuts):
        lanes = slice(cut * wide, (cut + 1) * wide)
        product = jnp.dot(mine, w_v[:, lanes], preferred_element_type=F32)
        upper, lower = product[:half], product[half:]
        part_own[:, lanes] = jnp.where(c == 0, upper, lower)
        part_send[cut] = jnp.where(c == 0, lower, upper).astype(BF16)
        put(part_send.at[cut], part_recv.at[cut], c_send.at[cut], c_sem.at[cut], AX_C, 1 - c)

    await_bytes(tbuf.at[0, 0:Z - 1], t2_sem)
    for hop in range(1, Y):
        put(tbuf.at[y], tbuf.at[y], t3_send, t3_sem.at[y], AX_Y, lax.rem(y + hop, Y))
    out_copies = [pltpu.make_async_copy(tbuf.at[y], t_out.at[y], local_sem.at[5])]
    out_copies[0].start()

    for cut in range(cuts):
        lanes = slice(cut * wide, (cut + 1) * wide)
        await_bytes(part_recv.at[cut], c_sem.at[cut])
        p_out[:, lanes] = part_own[:, lanes] + part_recv[cut].astype(F32)

    for hop in range(1, Y):
        other = lax.rem(y + hop, Y)
        await_bytes(tbuf.at[other], t3_sem.at[other])
        out = pltpu.make_async_copy(tbuf.at[other], t_out.at[other], local_sem.at[5 + hop])
        out.start()
        out_copies.append(out)

    await_bytes(send.at[0:Z - 1], z_send)
    await_bytes(kvg.at[0:Y - 1], ykv_send)
    await_bytes(qg.at[0:X - 1], xq_send)
    for hop in range(1, X):
        await_bytes(tob, xto_send.at[hop])
        await_bytes(tst, xts_send.at[hop])
        await_bytes(ob.at[0], xo_send.at[hop])
        await_bytes(st.at[0], xs_send.at[hop])
    await_bytes(zs.at[0:Z - 1], zo_send)
    await_bytes(tbuf.at[0, 0:Z - 1], t2_send)
    await_bytes(tbuf.at[0:Y - 1], t3_send)
    for cut in range(cuts):
        await_bytes(part_send.at[cut], c_send.at[cut])
    for out in out_copies:
        out.wait()


def shards(
    img_qkv, txt_qkv, frame_index, row_index, column_index, txt_len, residual, w_proj, proj_bias, gate,
):
    Z, X, Y = (lax.axis_size(a) for a in SEQ)
    tok = img_qkv.shape[1]
    width = img_qkv.shape[3]
    txt_total = txt_qkv.shape[1]
    out_width = w_proj.shape[1]
    txt_q, txt_k = txt_total // Y, txt_total // X
    cuts = 6
    wide = out_width // cuts
    half = tok // 2
    block_n = Z * tok
    strips = block_n // HD

    qkv = jnp.transpose(img_qkv[0], (1, 0, 2))
    txt = jnp.transpose(txt_qkv[0], (1, 0, 2))
    dma = pltpu.SemaphoreType.DMA
    vm = pltpu.VMEM
    any_spec = pl.BlockSpec(memory_space=pltpu.HBM)
    vmem_spec = pl.BlockSpec(memory_space=pltpu.VMEM)

    def body(*refs):
        kernel_body(Z, X, Y, tok, *refs)

    projected, txt_parts = pl.pallas_call(
        body,
        out_shape=(
            jax.ShapeDtypeStruct((half, out_width), F32),
            jax.ShapeDtypeStruct((Y, Z, txt_q, HD), BF16),
        ),
        in_specs=[any_spec] * 3 + [vmem_spec] * 3 + [pl.BlockSpec(memory_space=pltpu.SMEM)],
        out_specs=(vmem_spec, any_spec),
        scratch_shapes=[
            vm((3, tok, width), BF16),
            vm(w_proj.shape, BF16),
            vm((txt_q, HD), BF16), vm((txt_k, HD), BF16), vm((txt_k, HD), BF16),
            vm((Z, 3, tok, HD), BF16),
            vm((X, Z, tok, HD), BF16),
            vm((Y, Z, 2, tok, HD), BF16),
            vm((X, block_n, HD), BF16), vm((X, strips, 1, HD), F32),
            vm((X, block_n, HD), BF16), vm((X, strips, 1, HD), F32),
            vm((txt_q, HD), BF16), vm((1, HD), F32),
            vm((X, txt_q, HD), BF16), vm((X, 1, HD), F32),
            vm((Z, tok, HD), BF16), vm((Z, tok, HD), BF16),
            vm((Y, Z, txt_q, HD), BF16),
            vm((half, out_width), F32), vm((cuts, half, wide), BF16), vm((cuts, half, wide), BF16),
            dma((5 + Y,)), dma((Z,)), dma((Z,)), dma(()), dma((X,)), dma(()), dma((Y,)), dma(()),
            dma((X,)), dma((X,)), dma((X,)), dma((X,)), dma((X,)), dma((X,)), dma((X,)), dma((X,)),
            dma(()), dma(()), dma(()), dma(()), dma((Y,)), dma(()), dma((cuts,)), dma((cuts,)),
        ],
        compiler_params=pltpu.CompilerParams(
            collective_id=0, has_side_effects=True, vmem_limit_bytes=56 * 1024 * 1024),
        name="joint_attention",
    )(qkv, txt, w_proj, frame_index, row_index, column_index, txt_len)

    img_out = (
        residual.astype(F32) + gate[None, None, :] * (projected[None] + proj_bias[None, None, :])
    ).astype(BF16)
    txt_out = txt_parts.transpose(0, 2, 1, 3).reshape(1, txt_total, width)
    return (img_out, txt_out)


def solution(mesh):
    shape = getattr(mesh, "solution_shape", (8, 4, 4))
    split = Mesh(mesh.devices.reshape(*shape, mesh.shape["tp"]), SEQ_TP)
    placed = (
        P(None, SEQ, None, "tp"),
        P(None, None, None, "tp"),
        P(None, SEQ),
        P(None, SEQ),
        P(None, SEQ),
        P(),
        P(None, SEQ_TP, None),
        P("tp", None),
        P(),
        P(),
    )
    return jax.shard_map(
        shards,
        mesh=split,
        in_specs=placed,
        out_specs=(P(None, SEQ_TP, None), P(None, None, "tp")),
        check_vma=False,
    )
```

time: 181 us -> 47.8 us (0.26)
  the two profiles are of different devices: /device:TPU:1 before, /device:TPU:2 now
where the time goes in v1:
time: 47.8 us; the launch traced here: 47.6 us
  Pallas kernels  42.2 us (88%)
  local copies, waits for them, and re-layouts  2.41 us (5%)
  other arithmetic  1.6 us (3%)
  between operations  1.37 us (3%)
    pallas_call x1, Pallas kernels, shards(): pl.pallas_call(body, out_shape=(jax.ShapeDtypeStruct((half, out_width), F...  42.2 us
    convert_element_type x1, other arithmetic, shards(): img_out = (residual.astype(F32) + gate[None, None, :] * (projected[None]...  1.6 us
    transpose x1, local copies, waits for them, and re-layouts, shards(): txt_out = txt_parts.transpose(0, 2, 1, 3).reshape(1, txt_total, width)  1.38 us
    reshape x1, local copies, waits for them, and re-layouts, shards(): txt_out = txt_parts.transpose(0, 2, 1, 3).reshape(1, txt_total, width)  1.02 us

profile of v1, /device:TPU:2, one launch (start us, length us, event | category | flops | bytes accessed | tf_op | source)
XLA Modules:
  0.0 47.6 jit_solution(3323006817596679437)
XLA Ops:
  0.6 0.0 copy-start.2
  0.6 0.0 copy-start.1
  0.7 0.0 copy-start
  1.3 42.2 %joint_attention.1 = (f32[16,3072]{1,0:T(8,128)}, bf16[4,8,64,128]{3,2,1,0:T(8,128)(2,1)}) custom-call(bf16[3,32,1024]{2,1,0:T(8,128)(2,1)} %bitcast.15, bf16[3,256,1024]{2,1,0:T(8,128)(2,1)} %bitcast.13, bf16[1024,3072]{1,0:T(8,128)(2,1)} %refs_2_.1, s32[1,32]{1,0:T(1,128)} %refs_3_.1, s32[1,32]{1,0:T(1,128)} %refs_4_.1, s32[1,32]{1,0:T(1,128)} %refs_5_.1, ...), custom_call_target="tpu_custom_call" | custom-call | tf_op jit(solution)/shard_map/joint_attention/pallas_call | solution.py:293
  43.6 0.0 copy-done.2
  43.6 0.0 copy-done.1
  43.6 0.0 copy-done
  43.6 1.6 %fusion = bf16[1,16,3072]{2,1,0:T(8,128)(2,1)} fusion(f32[16,3072]{1,0:T(8,128)} %get-tuple-element.4, bf16[1,16,3072]{2,1,0:T(8,128)(2,1)S(1)} %copy-done, f32[3072]{0:T(1024)S(1)} %copy-done.1, f32[3072]{0:T(1024)S(1)} %copy-done.2), kind=kLoop, calls=%fused_computation.1 | loop fusion | flops 245760 | bytes 417792 | tf_op jit(solution)/shard_map/convert_element_type | solution.py:326
  45.2 1.4 %copy.12 = bf16[4,64,8,128]{3,2,1,0:T(8,128)(2,1)S(1)} copy(bf16[4,64,8,128]{3,1,2,0:T(8,128)(2,1)} %bitcast.14) | data formatting | bytes 1048576 | tf_op jit(solution)/shard_map/transpose | solution.py:327
  46.6 1.0 %reshape.15 = bf16[1,256,1024]{2,1,0:T(8,128)(2,1)} reshape(bf16[4,64,8,128]{3,2,1,0:T(8,128)(2,1)S(1)} %copy.12) | data formatting | bytes 1048576 | tf_op jit(solution)/shard_map/reshape | solution.py:327
Async XLA Ops:
  0.6 42.9 %copy-start.2 = (f32[3072]{0:T(1024)S(1)}, f32[3072]{0:T(1024)}, u32[]{:S(2)}) copy-start(f32[3072]{0:T(1024)} %param.19) | copy-start | bytes 36868
  0.6 42.9 %copy-start.1 = (f32[3072]{0:T(1024)S(1)}, f32[3072]{0:T(1024)}, u32[]{:S(2)}) copy-start(f32[3072]{0:T(1024)} %param.18) | copy-start | bytes 36868
  0.7 42.9 %copy-start = (bf16[1,16,3072]{2,1,0:T(8,128)(2,1)S(1)}, bf16[1,16,3072]{2,1,0:T(8,128)(2,1)}, u32[]{:S(2)}) copy-start(bf16[1,16,3072]{2,1,0:T(8,128)(2,1)} %param.16) | copy-start | bytes 294916

commit v2 on v1

v2 whole, which is shorter than its diff:
```python
import math

import jax
import jax.numpy as jnp
from jax import lax
from jax.experimental import pallas as pl
from jax.experimental.pallas import tpu as pltpu
from jax.sharding import Mesh
from jax.sharding import PartitionSpec as P

HD = 128
AX_Z, AX_X, AX_Y, AX_C = "seq_0", "seq_1", "seq_2", "tp"
SEQ = (AX_Z, AX_X, AX_Y)
SEQ_TP = (AX_Z, AX_X, AX_Y, AX_C)
MESH = pl.DeviceIdType.MESH
F32 = jnp.float32
BF16 = jnp.bfloat16

rope_base = 256.0
neg_large = -1e30


def rope_in_kernel(frames, rows, columns, tok):
    part0 = HD // 8
    part1 = (HD - part0) // 2
    eye = lax.broadcasted_iota(jnp.int32, (tok, tok), 0) == lax.broadcasted_iota(jnp.int32, (tok, tok), 1)

    def column(ref):
        places = jnp.broadcast_to(ref[...].astype(F32), (tok, tok))
        return jnp.sum(jnp.where(eye, places, 0.0), axis=1, keepdims=True)

    lane = lax.broadcasted_iota(jnp.int32, (tok, HD), 1)
    in0 = lane < part0
    in1 = lane < part0 + part1
    start = jnp.where(in0, 0, jnp.where(in1, part0, part0 + part1))
    pair = ((lane - start) >> 1).astype(F32)
    width = jnp.where(in0, float(part0), float(part1))
    rate = jnp.exp(pair * (-2.0 * math.log(rope_base)) / width)
    place = jnp.where(in0, column(frames), jnp.where(in1, column(rows), column(columns)))
    angle = place * rate
    cosine, sine = jnp.cos(angle), jnp.sin(angle)
    even = (lane & 1) == 0
    return cosine, jnp.where(even, -sine, 0.0), jnp.where(even, 0.0, sine)


def kernel_body(
    Z, A, tok,
    qkv_hbm, txt_hbm, w_hbm, frames_hbm, rows_hbm, columns_hbm, txt_len, res_hbm, bias_hbm, gate_hbm,
    img_out, txt_out,
    qkv_v, w_v, frames, rows, columns, res_v, bias_v, gate_v, tq, tk, tv,
    send, qg, kvg, acc, peak_s, sum_s, ob, st, orecv, srecv, tob, tst, torecv, tsrecv,
    zs, ar, tbuf, pacc, part_own, part_send, part_recv,
    local_sem, zq_sem, zkv_sem, z_send, aq_sem, aq_send, bkv_sem, bkv_send,
    ao_sem, as_sem, ao_send, as_send, ato_sem, ats_sem, ato_send, ats_send,
    zo_sem, zo_send, t2_sem, t2_send, t3_sem, t3_send, c_sem, c_send,
):
    z, x, y, c = (lax.axis_index(axis) for axis in SEQ_TP)
    B = A
    a = x * (1 - c) + y * c
    b = y * (1 - c) + x * c
    txt_n = tq.shape[0]
    scale2 = math.log2(math.e) / math.sqrt(HD)

    def along_a(to):
        return {AX_X: to * (1 - c) + x * c, AX_Y: y * (1 - c) + to * c}

    def along_b(to):
        return {AX_X: x * (1 - c) + to * c, AX_Y: to * (1 - c) + y * c}

    def put(src, dst, ssem, rsem, device):
        pltpu.make_async_remote_copy(
            src_ref=src, dst_ref=dst, send_sem=ssem, recv_sem=rsem, device_id=device, device_id_type=MESH,
        ).start()

    def await_bytes(ref, sem):
        pltpu.make_async_copy(ref, ref, sem).wait()

    barrier = pltpu.get_barrier_semaphore()
    peers = 0
    for axis, size, me in ((AX_Z, Z, z), (AX_X, A, x), (AX_Y, A, y), (AX_C, 2, c)):
        for step in range(1, size):
            pl.semaphore_signal(barrier, inc=1, device_id={axis: lax.rem(me + step, size)}, device_id_type=MESH)
            peers += 1

    lane0 = pl.multiple_of(z * HD, HD)
    rows_b = pl.ds(pl.multiple_of(b * txt_n, txt_n), txt_n)
    rows_a = pl.ds(pl.multiple_of(a * txt_n, txt_n), txt_n)
    gets = [
        pltpu.make_async_copy(src, dst, local_sem.at[i])
        for i, (src, dst) in enumerate((
            (frames_hbm, frames), (rows_hbm, rows), (columns_hbm, columns),
            (qkv_hbm, qkv_v),
            (txt_hbm.at[0, rows_b, pl.ds(lane0, HD)], tq),
            (txt_hbm.at[1, rows_a, pl.ds(lane0, HD)], tk.at[0:txt_n]),
            (txt_hbm.at[2, rows_a, pl.ds(lane0, HD)], tv.at[0:txt_n]),
            (bias_hbm, bias_v), (gate_hbm, gate_v), (res_hbm, res_v), (w_hbm, w_v),
        ))
    ]
    for get in gets:
        get.start()

    for get in gets[:3]:
        get.wait()
    cosine, sine_even, sine_odd = rope_in_kernel(frames, rows, columns, tok)
    gets[3].wait()
    for h in range(Z):
        lanes = slice(h * HD, (h + 1) * HD)
        for kind in range(2):
            block = qkv_v[kind, :, lanes].astype(F32)
            turned = (
                block * cosine
                + pltpu.roll(block, HD - 1, 1) * sine_even
                + pltpu.roll(block, 1, 1) * sine_odd
            )
            send[h, kind] = turned.astype(BF16)
        send[h, 2] = qkv_v[2, :, lanes]
    qg[a, z] = send[z, 0]
    kvg[b, z] = send[z, 1:3]

    pl.semaphore_wait(barrier, peers)

    far_first = sorted(range(1, Z), key=lambda step: -min(step, Z - step))
    near_first = sorted(range(1, Z), key=lambda step: min(step, Z - step))
    for step in far_first:
        to = lax.rem(z + step, Z)
        put(send.at[to, 0], qg.at[a, z], z_send, zq_sem.at[z], {AX_Z: to})
    for step in far_first:
        to = lax.rem(z + step, Z)
        put(send.at[to, 1:3], kvg.at[b, z], z_send, zkv_sem.at[z], {AX_Z: to})

    hops = sorted(range(1, A), key=lambda hop: -min(hop, A - hop))
    for step in [0] + near_first:
        source = lax.rem(z + step, Z)
        if step:
            with jax.named_scope(f"wait_zq{step}"):
                await_bytes(qg.at[a, source], zq_sem.at[source])
        for hop in hops:
            put(qg.at[a, source], qg.at[a, source], aq_send, aq_sem.at[a], along_a(lax.rem(a + hop, A)))
    for step in [0] + near_first:
        source = lax.rem(z + step, Z)
        if step:
            with jax.named_scope(f"wait_zkv{step}"):
                await_bytes(kvg.at[b, source], zkv_sem.at[source])
        for hop in hops:
            put(kvg.at[b, source], kvg.at[b, source], bkv_send, bkv_sem.at[b], along_b(lax.rem(b + hop, B)))

    block_n = Z * tok
    strips = block_n // HD
    pad = tk.shape[0] - txt_n
    if pad:
        tk[txt_n:] = jnp.zeros((pad, HD), BF16)
        tv[txt_n:] = jnp.zeros((pad, HD), BF16)
    for get in gets[4:7]:
        get.wait()
    length = txt_len[0]
    live = lax.broadcasted_iota(jnp.int32, (1, tk.shape[0]), 1) < jnp.minimum(length - a * txt_n, txt_n)

    def scores_of(queries, keys):
        return lax.dot_general(queries, keys, (((1,), (1,)), ((), ())), preferred_element_type=F32)

    def to_row(col):
        n = col.shape[0]
        eye = lax.broadcasted_iota(jnp.int32, (n, HD), 0) == lax.broadcasted_iota(jnp.int32, (n, HD), 1)
        return jnp.sum(jnp.where(eye, col, 0.0), axis=0, keepdims=True)

    def to_col(row, n):
        eye = lax.broadcasted_iota(jnp.int32, (n, HD), 0) == lax.broadcasted_iota(jnp.int32, (n, HD), 1)
        return jnp.sum(jnp.where(eye, jnp.broadcast_to(row, (n, HD)), 0.0), axis=1, keepdims=True)

    def wide(col):
        return jnp.broadcast_to(col, (col.shape[0], HD))

    def absorb(slot, n, queries, keys, values, first):
        at = slice(slot * block_n, slot * block_n + n)
        scores = scores_of(queries, keys)
        parts = [scores[:, i:i + HD] for i in range(0, keys.shape[0], HD)]
        if first:
            txt_scores = jnp.where(live, scores_of(queries, tk[...]), neg_large)
            parts += [txt_scores[:, i:i + HD] for i in range(0, tk.shape[0], HD)]
        top = parts[0]
        for part in parts[1:]:
            top = jnp.maximum(top, part)
        peak = wide(jnp.max(top, axis=1, keepdims=True))
        if not first:
            old = peak_s[at]
            peak = jnp.maximum(peak, old)
            shrink = jnp.exp2((old - peak) * scale2)
        weights = [jnp.exp2((part - peak) * scale2) for part in parts]
        total = weights[0]
        for weight in weights[1:]:
            total = total + weight
        weights = [weight.astype(BF16) for weight in weights]
        image_parts = keys.shape[0] // HD
        blended = jnp.dot(
            jnp.concatenate(weights[:image_parts], axis=1), values, preferred_element_type=F32)
        if first:
            blended = blended + jnp.dot(
                jnp.concatenate(weights[image_parts:], axis=1), tv[...], preferred_element_type=F32)
        else:
            total = total + sum_s[at] * shrink
            blended = blended + acc[at] * shrink
        return at, peak, total, blended

    key_hops = [0] + sorted(range(1, B), key=lambda hop: min(hop, B - hop))
    query_hops = hops + [0]
    arrived = set()
    for key_hop in key_hops:
        first, last = key_hop == key_hops[0], key_hop == key_hops[-1]
        other = lax.rem(b + key_hop, B)
        if not first:
            with jax.named_scope(f"wait_kv{key_hop}"):
                await_bytes(kvg.at[other], bkv_sem.at[other])
        keys = kvg[other, :, 0].reshape(block_n, HD)
        values = kvg[other, :, 1].reshape(block_n, HD)
        for hop in [None] + ([0] + hops[::-1] if first else query_hops):
            if hop is None:
                slot, n, queries = A, txt_n, tq[...]
            else:
                slot, n, to = hop, block_n, lax.rem(a + hop, A)
                if first and hop:
                    with jax.named_scope(f"wait_q{hop}"):
                        await_bytes(qg.at[to], aq_sem.at[to])
                queries = qg[to].reshape(block_n, HD)
            at, peak, total, blended = absorb(slot, n, queries, keys, values, first)
            if not last:
                peak_s[at], sum_s[at], acc[at] = peak, total, blended
                continue
            weight_sum = jnp.sum(total, axis=1, keepdims=True)
            result = (blended / weight_sum).astype(BF16)
            log = peak * scale2 + jnp.log2(weight_sum)
            if hop is None:
                tob[...] = result
                tst[...] = to_row(log)
                for via in hops:
                    dev = along_a(lax.rem(a + via, A))
                    put(tob, torecv.at[a], ato_send.at[via], ato_sem.at[a], dev)
                    put(tst, tsrecv.at[a], ats_send.at[via], ats_sem.at[a], dev)
                continue
            ob[hop] = result
            for strip in range(strips):
                st[hop, strip] = to_row(log[strip * HD:(strip + 1) * HD])
            if hop:
                put(ob.at[hop], orecv.at[a], ao_send.at[hop], ao_sem.at[a], along_a(to))
                put(st.at[hop], srecv.at[a], as_send.at[hop], as_sem.at[a], along_a(to))

    def merge(parts, logs):
        top = logs[0]
        for log in logs[1:]:
            top = jnp.maximum(top, log)
        shares = [jnp.exp2(log - top) for log in logs]
        return sum(part * share for part, share in zip(parts, shares)) / sum(shares)

    parts, logs = [tob[...].astype(F32)], [to_col(tst[...], txt_n)]
    for hop in hops[::-1]:
        other = lax.rem(a + hop, A)
        await_bytes(torecv.at[other], ato_sem.at[other])
        await_bytes(tsrecv.at[other], ats_sem.at[other])
        parts.append(torecv[other].astype(F32))
        logs.append(to_col(tsrecv[other], txt_n))
    kept = lax.broadcasted_iota(jnp.int32, (txt_n, 1), 0) + b * txt_n < length
    tbuf[b, z] = jnp.where(kept, merge(parts, logs), 0.0).astype(BF16)
    for step in far_first:
        put(tbuf.at[b, z], tbuf.at[b, z], t2_send, t2_sem.at[z], {AX_Z: lax.rem(z + step, Z)})

    for hop in hops:
        other = lax.rem(a + hop, A)
        await_bytes(orecv.at[other], ao_sem.at[other])
        await_bytes(srecv.at[other], as_sem.at[other])
    per = HD // tok
    for strip in range(strips):
        at = slice(strip * HD, (strip + 1) * HD)
        parts, logs = [ob[0, at].astype(F32)], [to_col(st[0, strip], HD)]
        for hop in hops:
            other = lax.rem(a + hop, A)
            parts.append(orecv[other, at].astype(F32))
            logs.append(to_col(srecv[other, strip], HD))
        zs[strip * per:(strip + 1) * per] = merge(parts, logs).astype(BF16).reshape(per, tok, HD)
    for step in far_first:
        to = lax.rem(z + step, Z)
        put(zs.at[to], ar.at[z], zo_send, zo_sem.at[z], {AX_Z: to})

    gets[-1].wait()
    half = tok // 2
    cuts = part_send.shape[0]
    width = part_send.shape[2]
    ar[z] = zs[z]
    for step in [0] + near_first:
        source = lax.rem(z + step, Z)
        if step:
            with jax.named_scope(f"wait_txt{step}"):
                await_bytes(tbuf.at[b, source], t2_sem.at[source])
        for hop in hops:
            put(tbuf.at[b, source], tbuf.at[b, source], t3_send, t3_sem.at[b], along_b(lax.rem(b + hop, B)))
        if step:
            with jax.named_scope(f"wait_home{step}"):
                await_bytes(ar.at[source], zo_sem.at[source])
        depth = pl.ds(pl.multiple_of(source * HD, HD), HD)
        for cut in range(cuts):
            lanes = slice(cut * width, (cut + 1) * width)
            product = jnp.dot(ar[source], w_v[depth, lanes], preferred_element_type=F32)
            if step:
                product = product + pacc[:, lanes]
            if step != near_first[-1]:
                pacc[:, lanes] = product
                continue
            upper, lower = product[:half], product[half:]
            part_own[:, lanes] = jnp.where(c == 0, upper, lower)
            part_send[cut] = jnp.where(c == 0, lower, upper).astype(BF16)
            put(part_send.at[cut], part_recv.at[cut], c_send.at[cut], c_sem.at[cut], {AX_C: 1 - c})

    for get in gets[7:10]:
        get.wait()
    for cut in range(cuts):
        lanes = slice(cut * width, (cut + 1) * width)
        await_bytes(part_recv.at[cut], c_sem.at[cut])
        projected = part_own[:, lanes] + part_recv[cut].astype(F32)
        img_out[:, lanes] = (
            res_v[:, lanes].astype(F32) + gate_v[:, lanes] * (projected + bias_v[:, lanes])
        ).astype(BF16)

    for hop in [0] + hops[::-1]:
        other = lax.rem(b + hop, B)
        if hop:
            await_bytes(tbuf.at[other], t3_sem.at[other])
        at = pl.ds(pl.multiple_of(other * txt_n, txt_n), txt_n)
        for h in range(Z):
            txt_out[at, h * HD:(h + 1) * HD] = tbuf[other, h]

    await_bytes(send.at[0:Z - 1], z_send)
    await_bytes(kvg.at[0:B - 1], bkv_send)
    await_bytes(qg.at[0:A - 1], aq_send)
    for hop in range(1, A):
        await_bytes(tob, ato_send.at[hop])
        await_bytes(tst, ats_send.at[hop])
        await_bytes(ob.at[hop], ao_send.at[hop])
        await_bytes(st.at[hop], as_send.at[hop])
    await_bytes(zs.at[0:Z - 1], zo_send)
    await_bytes(tbuf.at[0, 0:Z - 1], t2_send)
    await_bytes(tbuf.at[0:B - 1], t3_send)
    for cut in range(cuts):
        await_bytes(part_send.at[cut], c_send.at[cut])


def shards(
    img_qkv, txt_qkv, frame_index, row_index, column_index, txt_len, residual, w_proj, proj_bias, gate,
):
    Z, A, B = (lax.axis_size(axis) for axis in SEQ)
    tok = img_qkv.shape[1]
    width = img_qkv.shape[3]
    txt_total = txt_qkv.shape[1]
    out_width = w_proj.shape[1]
    txt_n = txt_total // A
    txt_pad = -(-txt_n // HD) * HD
    cuts = 6
    wide = out_width // cuts
    half = tok // 2
    block_n = Z * tok
    strips = block_n // HD
    rows_n = A * block_n + txt_n

    qkv = jnp.transpose(img_qkv[0], (1, 0, 2))
    txt = jnp.transpose(txt_qkv[0], (1, 0, 2))
    dma = pltpu.SemaphoreType.DMA
    vm = pltpu.VMEM
    hbm_spec = pl.BlockSpec(memory_space=pltpu.HBM)
    vmem_spec = pl.BlockSpec(memory_space=pltpu.VMEM)

    def body(*refs):
        kernel_body(Z, A, tok, *refs)

    img_v, txt_v = pl.pallas_call(
        body,
        out_shape=(pltpu.VMEM((half, out_width), BF16), pltpu.VMEM((txt_total, width), BF16)),
        in_specs=[hbm_spec] * 6 + [pl.BlockSpec(memory_space=pltpu.SMEM)] + [hbm_spec] * 3,
        out_specs=(vmem_spec, vmem_spec),
        scratch_shapes=[
            vm((3, tok, width), BF16),
            vm(w_proj.shape, BF16),
            vm((1, tok), jnp.int32), vm((1, tok), jnp.int32), vm((1, tok), jnp.int32),
            vm((half, out_width), BF16), vm((1, out_width), F32), vm((1, out_width), F32),
            vm((txt_n, HD), BF16), vm((txt_pad, HD), BF16), vm((txt_pad, HD), BF16),
            vm((Z, 3, tok, HD), BF16),
            vm((A, Z, tok, HD), BF16),
            vm((B, Z, 2, tok, HD), BF16),
            vm((rows_n, HD), F32), vm((rows_n, HD), F32), vm((rows_n, HD), F32),
            vm((A, block_n, HD), BF16), vm((A, strips, 1, HD), F32),
            vm((A, block_n, HD), BF16), vm((A, strips, 1, HD), F32),
            vm((txt_n, HD), BF16), vm((1, HD), F32),
            vm((A, txt_n, HD), BF16), vm((A, 1, HD), F32),
            vm((Z, tok, HD), BF16), vm((Z, tok, HD), BF16),
            vm((B, Z, txt_n, HD), BF16),
            vm((tok, out_width), F32),
            vm((half, out_width), F32), vm((cuts, half, wide), BF16), vm((cuts, half, wide), BF16),
            dma((11,)), dma((Z,)), dma((Z,)), dma(()), dma((A,)), dma(()), dma((B,)), dma(()),
            dma((A,)), dma((A,)), dma((A,)), dma((A,)), dma((A,)), dma((A,)), dma((A,)), dma((A,)),
            dma((Z,)), dma(()), dma((Z,)), dma(()), dma((B,)), dma(()), dma((cuts,)), dma((cuts,)),
        ],
        compiler_params=pltpu.CompilerParams(
            collective_id=0, has_side_effects=True, vmem_limit_bytes=24 * 1024 * 1024),
        name="joint_attention",
    )(*(
        operand if operand is txt_len else pltpu.with_memory_space_constraint(operand, pltpu.HBM)
        for operand in (
            qkv, txt, w_proj, frame_index, row_index, column_index, txt_len, residual[0],
            proj_bias.reshape(1, -1), gate.reshape(1, -1),
        )
    ))

    def write_out(img_ref, txt_ref, img_hbm, txt_hbm, sems):
        outs = [
            pltpu.make_async_copy(img_ref, img_hbm, sems.at[0]),
            pltpu.make_async_copy(txt_ref, txt_hbm, sems.at[1]),
        ]
        for out in outs:
            out.start()
        for out in outs:
            out.wait()

    img_out, txt_out = pl.pallas_call(
        write_out,
        out_shape=(
            jax.ShapeDtypeStruct((half, out_width), BF16),
            jax.ShapeDtypeStruct((txt_total, width), BF16),
        ),
        in_specs=[vmem_spec] * 2,
        out_specs=(hbm_spec, hbm_spec),
        scratch_shapes=[dma((2,))],
        compiler_params=pltpu.CompilerParams(vmem_limit_bytes=1024 * 1024),
        name="write_out",
    )(img_v, txt_v)
    return (img_out[None], txt_out[None])


def solution(mesh):
    shape = getattr(mesh, "solution_shape", (8, 4, 4))
    split = Mesh(mesh.devices.reshape(*shape, mesh.shape["tp"]), SEQ_TP)
    placed = (
        P(None, SEQ, None, "tp"),
        P(None, None, None, "tp"),
        P(None, SEQ),
        P(None, SEQ),
        P(None, SEQ),
        P(),
        P(None, SEQ_TP, None),
        P("tp", None),
        P(),
        P(),
    )
    return jax.shard_map(
        shards,
        mesh=split,
        in_specs=placed,
        out_specs=(P(None, SEQ_TP, None), P(None, None, "tp")),
        check_vma=False,
    )
```

time: 47.8 us -> 40.2 us (0.84)
  the two profiles are of different devices: /device:TPU:2 before, /device:TPU:1 now
where the time goes in v2:
time: 40.2 us; the launch traced here: 39.5 us
  Pallas kernels  38.2 us (95%)
  between operations  1.29 us (3%)
    pallas_call x1, Pallas kernels, shards(): pl.pallas_call(body, out_shape=(pltpu.VMEM((half, out_width), BF16), pltp...  37.4 us
    pallas_call x1, Pallas kernels, shards(): pl.pallas_call(write_out, out_shape=(jax.ShapeDtypeStruct((half, out_widt...  0.85 us

profile of v2, /device:TPU:1, one launch (start us, length us, event | category | flops | bytes accessed | tf_op | source)
XLA Modules:
  0.0 39.5 jit_solution(16024747042575245656)
XLA Ops:
  1.3 37.4 %joint_attention.1 = (bf16[16,3072]{1,0:T(8,128)(2,1)S(1)}, bf16[256,1024]{1,0:T(8,128)(2,1)S(1)}) custom-call(bf16[3,32,1024]{2,1,0:T(8,128)(2,1)} %bitcast.12, bf16[3,256,1024]{2,1,0:T(8,128)(2,1)} %bitcast.11, bf16[1024,3072]{1,0:T(8,128)(2,1)} %refs_2_.1, s32[1,32]{1,0:T(1,128)} %refs_3_.1, s32[1,32]{1,0:T(1,128)} %refs_4_.1, s32[1,32]{1,0:T(1,128)} %refs_5_.1, ...), custom_call_target="tpu_custom_call" | custom-call | tf_op jit(solution)/shard_map/joint_attention/pallas_call | solution.py:371
  38.7 0.8 %write_out.1 = (bf16[16,3072]{1,0:T(8,128)(2,1)}, bf16[256,1024]{1,0:T(8,128)(2,1)}) custom-call(bf16[16,3072]{1,0:T(8,128)(2,1)S(1)} %get-tuple-element.6.img_ref, bf16[256,1024]{1,0:T(8,128)(2,1)S(1)} %get-tuple-element.7.txt_ref), custom_call_target="tpu_custom_call" | custom-call | tf_op jit(solution)/shard_map/write_out/pallas_call | solution.py:419

commit v3 on v2

--- a/solution.py
+++ b/solution.py
@@ -50,9 +50,8 @@
     qkv_v, w_v, frames, rows, columns, res_v, bias_v, gate_v, tq, tk, tv,
     send, qg, kvg, acc, peak_s, sum_s, ob, st, orecv, srecv, tob, tst, torecv, tsrecv,
     zs, ar, tbuf, pacc, part_own, part_send, part_recv,
-    local_sem, zq_sem, zkv_sem, z_send, aq_sem, aq_send, bkv_sem, bkv_send,
-    ao_sem, as_sem, ao_send, as_send, ato_sem, ats_sem, ato_send, ats_send,
-    zo_sem, zo_send, t2_sem, t2_send, t3_sem, t3_send, c_sem, c_send,
+    local_sem, zq_sem, zkv_sem, aq_sem, bkv_sem, ao_sem, as_sem, ato_sem, ats_sem,
+    zo_sem, t2_sem, t3_sem, c_sem, send_sem, log_send,
 ):
     z, x, y, c = (lax.axis_index(axis) for axis in SEQ_TP)
     B = A
@@ -119,30 +118,36 @@
 
     pl.semaphore_wait(barrier, peers)
 
+    def apart(step):
+        return min(step, Z - step) - 1
+
+    pairs = [[0]] + [sorted({d, Z - d}) for d in range(1, Z // 2 + 1)]
     far_first = sorted(range(1, Z), key=lambda step: -min(step, Z - step))
     near_first = sorted(range(1, Z), key=lambda step: min(step, Z - step))
     for step in far_first:
         to = lax.rem(z + step, Z)
-        put(send.at[to, 0], qg.at[a, z], z_send, zq_sem.at[z], {AX_Z: to})
+        put(send.at[to, 0], qg.at[a, z], send_sem, zq_sem.at[apart(step)], {AX_Z: to})
     for step in far_first:
         to = lax.rem(z + step, Z)
-        put(send.at[to, 1:3], kvg.at[b, z], z_send, zkv_sem.at[z], {AX_Z: to})
+        put(send.at[to, 1:3], kvg.at[b, z], send_sem, zkv_sem.at[apart(step)], {AX_Z: to})
 
     hops = sorted(range(1, A), key=lambda hop: -min(hop, A - hop))
-    for step in [0] + near_first:
-        source = lax.rem(z + step, Z)
-        if step:
-            with jax.named_scope(f"wait_zq{step}"):
-                await_bytes(qg.at[a, source], zq_sem.at[source])
-        for hop in hops:
-            put(qg.at[a, source], qg.at[a, source], aq_send, aq_sem.at[a], along_a(lax.rem(a + hop, A)))
-    for step in [0] + near_first:
-        source = lax.rem(z + step, Z)
-        if step:
-            with jax.named_scope(f"wait_zkv{step}"):
-                await_bytes(kvg.at[b, source], zkv_sem.at[source])
-        for hop in hops:
-            put(kvg.at[b, source], kvg.at[b, source], bkv_send, bkv_sem.at[b], along_b(lax.rem(b + hop, B)))
+    for pair in pairs:
+        if pair[0]:
+            with jax.named_scope(f"wait_zq{pair[0]}"):
+                await_bytes(qg.at[a, 0:len(pair)], zq_sem.at[apart(pair[0])])
+        for step in pair:
+            source = lax.rem(z + step, Z)
+            for hop in hops:
+                put(qg.at[a, source], qg.at[a, source], send_sem, aq_sem, along_a(lax.rem(a + hop, A)))
+    for pair in pairs:
+        if pair[0]:
+            with jax.named_scope(f"wait_zkv{pair[0]}"):
+                await_bytes(kvg.at[b, 0:len(pair)], zkv_sem.at[apart(pair[0])])
+        for step in pair:
+            source = lax.rem(z + step, Z)
+            for hop in hops:
+                put(kvg.at[b, source], kvg.at[b, source], send_sem, bkv_sem.at[hop], along_b(lax.rem(b + hop, B)))
 
     block_n = Z * tok
     strips = block_n // HD
@@ -170,8 +175,17 @@
     def wide(col):
         return jnp.broadcast_to(col, (col.shape[0], HD))
 
-    def absorb(slot, n, queries, keys, values, first):
-        at = slice(slot * block_n, slot * block_n + n)
+    def rows_of(hop, to_hop=None):
+        to_hop = hop if to_hop is None else to_hop
+        return slice(txt_n + hop * block_n, txt_n + (to_hop + 1) * block_n)
+
+    txt_rows = slice(0, txt_n)
+
+    def image_queries(*hop_list):
+        return [qg[lax.rem(a + hop, A)].reshape(block_n, HD) for hop in hop_list]
+
+    def absorb(at, queries, keys, values, first):
+        queries = jnp.concatenate(queries, axis=0) if len(queries) > 1 else queries[0]
         scores = scores_of(queries, keys)
         parts = [scores[:, i:i + HD] for i in range(0, keys.shape[0], HD)]
         if first:
@@ -199,49 +213,62 @@
         else:
             total = total + sum_s[at] * shrink
             blended = blended + acc[at] * shrink
-        return at, peak, total, blended
+        return peak, total, blended
+
+    def finish(state):
+        peak, total, blended = state
+        weight_sum = jnp.sum(total, axis=1, keepdims=True)
+        return (blended / weight_sum).astype(BF16), peak * scale2 + jnp.log2(weight_sum)
+
+    def finish_image(lo, hi, keys, values):
+        result, log = finish(
+            absorb(rows_of(lo, hi), image_queries(*range(lo, hi + 1)), keys, values, False))
+        for hop in range(lo, hi + 1):
+            base = (hop - lo) * block_n
+            ob[hop] = result[base:base + block_n]
+            for strip in range(strips):
+                st[hop, strip] = to_row(log[base + strip * HD:base + (strip + 1) * HD])
+
+    def keep(at, state):
+        peak_s[at], sum_s[at], acc[at] = state
 
     key_hops = [0] + sorted(range(1, B), key=lambda hop: min(hop, B - hop))
-    query_hops = hops + [0]
-    arrived = set()
+    all_rows = slice(0, txt_n + A * block_n)
     for key_hop in key_hops:
         first, last = key_hop == key_hops[0], key_hop == key_hops[-1]
         other = lax.rem(b + key_hop, B)
         if not first:
             with jax.named_scope(f"wait_kv{key_hop}"):
-                await_bytes(kvg.at[other], bkv_sem.at[other])
+                await_bytes(kvg.at[other], bkv_sem.at[B - key_hop])
         keys = kvg[other, :, 0].reshape(block_n, HD)
         values = kvg[other, :, 1].reshape(block_n, HD)
-        for hop in [None] + ([0] + hops[::-1] if first else query_hops):
-            if hop is None:
-                slot, n, queries = A, txt_n, tq[...]
-            else:
-                slot, n, to = hop, block_n, lax.rem(a + hop, A)
-                if first and hop:
-                    with jax.named_scope(f"wait_q{hop}"):
-                        await_bytes(qg.at[to], aq_sem.at[to])
-                queries = qg[to].reshape(block_n, HD)
-            at, peak, total, blended = absorb(slot, n, queries, keys, values, first)
-            if not last:
-                peak_s[at], sum_s[at], acc[at] = peak, total, blended
-                continue
-            weight_sum = jnp.sum(total, axis=1, keepdims=True)
-            result = (blended / weight_sum).astype(BF16)
-            log = peak * scale2 + jnp.log2(weight_sum)
-            if hop is None:
-                tob[...] = result
-                tst[...] = to_row(log)
-                for via in hops:
-                    dev = along_a(lax.rem(a + via, A))
-                    put(tob, torecv.at[a], ato_send.at[via], ato_sem.at[a], dev)
-                    put(tst, tsrecv.at[a], ats_send.at[via], ats_sem.at[a], dev)
-                continue
-            ob[hop] = result
-            for strip in range(strips):
-                st[hop, strip] = to_row(log[strip * HD:(strip + 1) * HD])
-            if hop:
-                put(ob.at[hop], orecv.at[a], ao_send.at[hop], ao_sem.at[a], along_a(to))
-                put(st.at[hop], srecv.at[a], as_send.at[hop], as_sem.at[a], along_a(to))
+        if first:
+            near_rows, far_rows = slice(0, txt_n + block_n), rows_of(1, A - 1)
+            keep(near_rows, absorb(near_rows, [tq[...]] + image_queries(0), keys, values, True))
+            with jax.named_scope("wait_q"):
+                await_bytes(qg.at[0:A - 1], aq_sem)
+            keep(far_rows, absorb(far_rows, image_queries(*range(1, A)), keys, values, True))
+        elif not last:
+            keep(all_rows, absorb(
+                all_rows, [tq[...]] + image_queries(*range(A)), keys, values, False))
+    result, log = finish(absorb(txt_rows, [tq[...]], keys, values, False))
+    tob[...], tst[...] = result, to_row(log)
+    for hop in hops:
+        to = along_a(lax.rem(a + hop, A))
+        put(tob, torecv.at[a], send_sem, ato_sem, to)
+        put(tst, tsrecv.at[a], log_send.at[0], ats_sem, to)
+    finish_image(1, A - 1, keys, values)
+    for hop in hops:
+        to = along_a(lax.rem(a + hop, A))
+        put(ob.at[hop], orecv.at[a], send_sem, ao_sem, to)
+        put(st.at[hop], srecv.at[a], log_send.at[1], as_sem, to)
+    finish_image(0, 0, keys, values)
+
+    others_up = [i + jnp.where(z <= i, 1, 0) for i in range(Z - 1)]
+
+    def far(to):
+        gap = lax.rem(to - z + Z, Z)
+        return jnp.minimum(gap, Z - gap) - 1
 
     def merge(parts, logs):
         top = logs[0]
@@ -250,22 +277,20 @@
         shares = [jnp.exp2(log - top) for log in logs]
         return sum(part * share for part, share in zip(parts, shares)) / sum(shares)
 
+    await_bytes(torecv.at[0:A - 1], ato_sem)
+    await_bytes(tsrecv.at[0:A - 1], ats_sem)
     parts, logs = [tob[...].astype(F32)], [to_col(tst[...], txt_n)]
     for hop in hops[::-1]:
         other = lax.rem(a + hop, A)
-        await_bytes(torecv.at[other], ato_sem.at[other])
-        await_bytes(tsrecv.at[other], ats_sem.at[other])
         parts.append(torecv[other].astype(F32))
         logs.append(to_col(tsrecv[other], txt_n))
     kept = lax.broadcasted_iota(jnp.int32, (txt_n, 1), 0) + b * txt_n < length
     tbuf[b, z] = jnp.where(kept, merge(parts, logs), 0.0).astype(BF16)
-    for step in far_first:
-        put(tbuf.at[b, z], tbuf.at[b, z], t2_send, t2_sem.at[z], {AX_Z: lax.rem(z + step, Z)})
-
-    for hop in hops:
-        other = lax.rem(a + hop, A)
-        await_bytes(orecv.at[other], ao_sem.at[other])
-        await_bytes(srecv.at[other], as_sem.at[other])
+    for to in others_up:
+        put(tbuf.at[b, z], tbuf.at[b, z], send_sem, t2_sem.at[far(to)], {AX_Z: to})
+
+    await_bytes(orecv.at[0:A - 1], ao_sem)
+    await_bytes(srecv.at[0:A - 1], as_sem)
     per = HD // tok
     for strip in range(strips):
         at = slice(strip * HD, (strip + 1) * HD)
@@ -275,70 +300,78 @@
             parts.append(orecv[other, at].astype(F32))
             logs.append(to_col(srecv[other, strip], HD))
         zs[strip * per:(strip + 1) * per] = merge(parts, logs).astype(BF16).reshape(per, tok, HD)
-    for step in far_first:
-        to = lax.rem(z + step, Z)
-        put(zs.at[to], ar.at[z], zo_send, zo_sem.at[z], {AX_Z: to})
+    for to in others_up:
+        put(zs.at[to], ar.at[z], send_sem, zo_sem.at[far(to)], {AX_Z: to})
 
     gets[-1].wait()
     half = tok // 2
     cuts = part_send.shape[0]
     width = part_send.shape[2]
     ar[z] = zs[z]
-    for step in [0] + near_first:
+    def text_on(pair):
+        if pair[0]:
+            with jax.named_scope(f"wait_txt{pair[0]}"):
+                await_bytes(tbuf.at[b, 0:len(pair)], t2_sem.at[apart(pair[0])])
+        for step in pair:
+            source = lax.rem(z + step, Z)
+            for hop in hops:
+                put(tbuf.at[b, source], tbuf.at[b, source], send_sem, t3_sem, along_b(lax.rem(b + hop, B)))
+
+    def project(step):
         source = lax.rem(z + step, Z)
-        if step:
-            with jax.named_scope(f"wait_txt{step}"):
-                await_bytes(tbuf.at[b, source], t2_sem.at[source])
-        for hop in hops:
-            put(tbuf.at[b, source], tbuf.at[b, source], t3_send, t3_sem.at[b], along_b(lax.rem(b + hop, B)))
-        if step:
-            with jax.named_scope(f"wait_home{step}"):
-                await_bytes(ar.at[source], zo_sem.at[source])
         depth = pl.ds(pl.multiple_of(source * HD, HD), HD)
         for cut in range(cuts):
             lanes = slice(cut * width, (cut + 1) * width)
             product = jnp.dot(ar[source], w_v[depth, lanes], preferred_element_type=F32)
             if step:
                 product = product + pacc[:, lanes]
-            if step != near_first[-1]:
+            if step != pairs[-1][-1]:
                 pacc[:, lanes] = product
                 continue
             upper, lower = product[:half], product[half:]
             part_own[:, lanes] = jnp.where(c == 0, upper, lower)
             part_send[cut] = jnp.where(c == 0, lower, upper).astype(BF16)
-            put(part_send.at[cut], part_recv.at[cut], c_send.at[cut], c_sem.at[cut], {AX_C: 1 - c})
+            put(part_send.at[cut], part_recv.at[cut], send_sem, c_sem.at[cut // 2], {AX_C: 1 - c})
+
+    def home(pair):
+        if pair[0]:
+            with jax.named_scope(f"wait_home{pair[0]}"):
+                await_bytes(ar.at[0:len(pair)], zo_sem.at[apart(pair[0])])
+        for step in pair:
+            project(step)
+
+    text_on(pairs[0])
+    home(pairs[0])
+    text_on(pairs[1])
+    for pair, behind in zip(pairs[2:], pairs[1:]):
+        text_on(pair)
+        home(behind)
+    home(pairs[-1])
 
     for get in gets[7:10]:
         get.wait()
     for cut in range(cuts):
         lanes = slice(cut * width, (cut + 1) * width)
-        await_bytes(part_recv.at[cut], c_sem.at[cut])
+        if cut % 2 == 0:
+            await_bytes(part_recv.at[cut:cut + 2], c_sem.at[cut // 2])
         projected = part_own[:, lanes] + part_recv[cut].astype(F32)
         img_out[:, lanes] = (
             res_v[:, lanes].astype(F32) + gate_v[:, lanes] * (projected + bias_v[:, lanes])
         ).astype(BF16)
 
-    for hop in [0] + hops[::-1]:
-        other = lax.rem(b + hop, B)
-        if hop:
-            await_bytes(tbuf.at[other], t3_sem.at[other])
-        at = pl.ds(pl.multiple_of(other * txt_n, txt_n), txt_n)
+    await_bytes(tbuf.at[0:B - 1], t3_sem)
+    for part in range(B):
         for h in range(Z):
-            txt_out[at, h * HD:(h + 1) * HD] = tbuf[other, h]
-
-    await_bytes(send.at[0:Z - 1], z_send)
-    await_bytes(kvg.at[0:B - 1], bkv_send)
-    await_bytes(qg.at[0:A - 1], aq_send)
-    for hop in range(1, A):
-        await_bytes(tob, ato_send.at[hop])
-        await_bytes(tst, ats_send.at[hop])
-        await_bytes(ob.at[hop], ao_send.at[hop])
-        await_bytes(st.at[hop], as_send.at[hop])
-    await_bytes(zs.at[0:Z - 1], zo_send)
-    await_bytes(tbuf.at[0, 0:Z - 1], t2_send)
-    await_bytes(tbuf.at[0:B - 1], t3_send)
-    for cut in range(cuts):
-        await_bytes(part_send.at[cut], c_send.at[cut])
+            txt_out[part * txt_n:(part + 1) * txt_n, h * HD:(h + 1) * HD] = tbuf[part, h]
+
+    sent = (
+        (Z - 1) * math.prod(send.shape[1:]) + (A - 1) * math.prod(qg.shape[1:]) + (B - 1) * math.prod(kvg.shape[1:]) + (A - 1) * (math.prod(tob.shape) + math.prod(ob.shape[1:]))
+        + (Z - 1) * (math.prod(tbuf.shape[2:]) + math.prod(zs.shape[1:])) + (B - 1) * math.prod(tbuf.shape[1:]) + math.prod(part_send.shape)
+    )
+    assert sent % w_v.shape[1] == 0
+    await_bytes(w_v.at[0:sent // w_v.shape[1]], send_sem)
+    await_bytes(tsrecv.at[0:A - 1], log_send.at[0])
+    await_bytes(st.at[0:A - 1], log_send.at[1])
 
 
 def shards(
@@ -391,9 +424,8 @@
             vm((B, Z, txt_n, HD), BF16),
             vm((tok, out_width), F32),
             vm((half, out_width), F32), vm((cuts, half, wide), BF16), vm((cuts, half, wide), BF16),
-            dma((11,)), dma((Z,)), dma((Z,)), dma(()), dma((A,)), dma(()), dma((B,)), dma(()),
-            dma((A,)), dma((A,)), dma((A,)), dma((A,)), dma((A,)), dma((A,)), dma((A,)), dma((A,)),
-            dma((Z,)), dma(()), dma((Z,)), dma(()), dma((B,)), dma(()), dma((cuts,)), dma((cuts,)),
+            dma((11,)), dma((Z // 2,)), dma((Z // 2,)), dma(()), dma((B,)), dma(()), dma(()), dma(()), dma(()),
+            dma((Z // 2,)), dma((Z // 2,)), dma(()), dma((cuts // 2,)), dma(()), dma((2,)),
         ],
         compiler_params=pltpu.CompilerParams(
             collective_id=0, has_side_effects=True, vmem_limit_bytes=24 * 1024 * 1024),

time: 40.2 us -> 38.3 us (0.953); the launches traced: 39.5 us -> 38.2 us
  Pallas kernels: 38.2 us -> 36.9 us
    pallas_call x1, Pallas kernels: 37.4 us -> 36.1 us  [shards(): pl.pallas_call(body, out_shape=(pltpu.VMEM((half, out_width), BF16), pltp...]
where the time goes in v3:
time: 38.3 us; the launch traced here: 38.2 us
  Pallas kernels  36.9 us (96%)
  between operations  1.29 us (3%)
    pallas_call x1, Pallas kernels, shards(): pl.pallas_call(body, out_shape=(pltpu.VMEM((half, out_width), BF16), pltp...  36.1 us
    pallas_call x1, Pallas kernels, shards(): pl.pallas_call(write_out, out_shape=(jax.ShapeDtypeStruct((half, out_widt...  0.85 us

profile of v3, /device:TPU:1, one launch (start us, length us, event | category | flops | bytes accessed | tf_op | source)
XLA Modules:
  0.0 38.2 jit_solution(5291895108230077162)
XLA Ops:
  1.3 36.1 %joint_attention.1 = (bf16[16,3072]{1,0:T(8,128)(2,1)S(1)}, bf16[256,1024]{1,0:T(8,128)(2,1)S(1)}) custom-call(bf16[3,32,1024]{2,1,0:T(8,128)(2,1)} %bitcast.12, bf16[3,256,1024]{2,1,0:T(8,128)(2,1)} %bitcast.11, bf16[1024,3072]{1,0:T(8,128)(2,1)} %refs_2_.1, s32[1,32]{1,0:T(1,128)} %refs_3_.1, s32[1,32]{1,0:T(1,128)} %refs_4_.1, s32[1,32]{1,0:T(1,128)} %refs_5_.1, ...), custom_call_target="tpu_custom_call" | custom-call | tf_op jit(solution)/shard_map/joint_attention/pallas_call | solution.py:404
  37.4 0.8 %write_out.1 = (bf16[16,3072]{1,0:T(8,128)(2,1)}, bf16[256,1024]{1,0:T(8,128)(2,1)}) custom-call(bf16[16,3072]{1,0:T(8,128)(2,1)S(1)} %get-tuple-element.6.img_ref, bf16[256,1024]{1,0:T(8,128)(2,1)S(1)} %get-tuple-element.7.txt_ref), custom_call_target="tpu_custom_call" | custom-call | tf_op jit(solution)/shard_map/write_out/pallas_call | solution.py:451
